TPU v7x, 32 devices: a whole 2x2x4 slice. The times are simulated.
32 devices in a mesh: member: 2 (over y), win: 4 (over z), seq: 4 (over x, core).
Axes of the slice: x: 2, y: 2, z: 4, core: 2. Of those that a mesh axis runs over, the one named last changes fastest.
Arguments:
- pixel_grid_input: bfloat16 [8, 8, 4, 64, 1536], P(('member', 'win'), None, 'seq'), parts along dimension 0, may hold values from -6 to 6
- mask_zone_labeling: int32 [8, 32, 64], P(('member', 'win')), parts along dimension 0, may hold values from 0 to 8, as said below
- standardize_multiplier: float32 [1536], replicated, may hold values from 0.25 to 1.75
- standardize_offset_vector: float32 [1536], replicated, may hold values from -3 to 3
- triple_projection_matrix: bfloat16 [3, 1536, 1536], P(None, None, 'seq'), may hold values from -0.15625 to 0.15625
- logit_scaling_per_part: float32 [16], P('seq'), may hold values from 1 to 45
- final_projection_matrix: bfloat16 [1536, 1536], P('seq'), may hold values from -0.15625 to 0.15625
Outputs:
- mixed: bfloat16 [8, 8, 4, 64, 1536], P(('member', 'win'), None, 'seq'), parts along dimension 0
There are 2 independent parts, one for each index of `member`. A program takes and returns all parts, laid end to end along the dimension named above; an argument that names none is the same for every part. Nothing has to cross between parts.
Inputs may be any that keep to these rules, and one draw needn't show every extreme that they name: `mask_zone_labeling`: region is 3 * (row band) + (column band) of the pixel on the rolled grid: the row band is 0 in the first 32 rows, 1 in the next rows and 2 in the last few rows, whose count is drawn once for each member from 4 to 27; the column bands are cut the same way within the last 32 columns of the grid, with a count drawn apart. Only windows in the last window row or the last window column of the grid hold more than one region.
All inputs are finite; a program needn't handle non-finite values.
Results may differ from a plain program's by a relative error of at most 0.0065.
The roundings to bfloat16 on the way count: a program that leaves them out, or rounds other values in their place, can miss the bound.
Values may be sent and summed in bfloat16 or wider, within the bound.
A program may use at most 64 MiB of HBM per device.

v0:
```python
import functools
import math

import jax
import jax.numpy as jnp
from jax import lax
from jax.experimental import pallas as pl
from jax.experimental.pallas import tpu as pltpu
from jax.sharding import PartitionSpec as P

CHANNEL_PER_PART = 96
PADDED = 128
WS = 32
HALF = WS // 2
LOG2E = 1.4426950408889634
MESH = pl.DeviceIdType.MESH


def xor(value, mask, bits):
    both = 0
    for b in range(bits):
        both = both + (1 << b) * ((value // (1 << b)) % 2) * ((mask // (1 << b)) % 2)
    return value + mask - 2 * both


def flip(value):
    return value + 1 - 2 * (value % 2)


def children(slot, lanes):
    low = lanes if slot == 0 else slot & -slot
    masks = [1 << b for b in reversed(range(lanes.bit_length() - 1))]
    return [slot | m for m in masks if m < low]


def layer_kernel(
    lanes,
    blocks,
    members,
    scale_ref,
    x_ref,
    label_ref,
    gain_ref,
    bias_ref,
    wqkv_ref,
    wout_ref,
    out_ref,
    pix,
    nrm,
    raw,
    wpad,
    wall,
    qkv,
    extq,
    extk,
    labt,
    att_out,
    att_in,
    acc,
    obuf,
    fetch_send,
    fetch_recv,
    norm_send,
    norm_recv,
    att_send,
    att_recv,
    w_send,
    w_recv,
    local_sem,
    out_sem,
):
    me = lax.axis_index("seq")
    win = lax.axis_index("win")
    member = lax.axis_index("member")
    bits = lanes.bit_length() - 1
    pieces, step, _, width = pix.shape
    rows = 2 * step
    group = step * HALF
    chunk = 4 * group
    window_count = pieces // 4
    head_width = att_out.shape[3]
    heads = head_width // CHANNEL_PER_PART
    cols = window_count * WS

    def at_seq(mask):
        return {"seq": xor(me, mask, bits)}

    def source(i):
        window, place, side = i // 4, (i // 2) % 2, i % 2
        first = window * WS + HALF + side * HALF
        span = pl.ds(step, step) if place == 0 else pl.ds(0, step)
        return place, first, x_ref.at[0, span, 0, pl.ds(first % cols, HALF), :]

    west = (win + blocks - 2) % blocks
    fetches = []
    locals_ = []
    for i in range(pieces):
        place, first, src = source(i)
        if place == 0 and first < cols:
            locals_.append(pltpu.make_async_copy(src, pix.at[i], fetch_recv.at[i]))
            continue
        if first < cols:
            to = flip(win)
        else:
            to = west if place == 0 else flip(west)
        fetches.append(
            pltpu.make_async_remote_copy(
                src_ref=src,
                dst_ref=pix.at[i],
                send_sem=fetch_send.at[i],
                recv_sem=fetch_recv.at[i],
                device_id={"win": to},
                device_id_type=MESH,
            )
        )

    def gather_copy(slot, i):
        parent = slot & (slot - 1)
        return pltpu.make_async_remote_copy(
            src_ref=nrm.at[parent, i],
            dst_ref=nrm.at[slot, i],
            send_sem=norm_send.at[slot, i],
            recv_sem=norm_recv.at[slot, i],
            device_id=at_seq(slot ^ parent),
            device_id_type=MESH,
        )

    def attended_copy(window, k):
        return pltpu.make_async_remote_copy(
            src_ref=att_out.at[window, k],
            dst_ref=att_in.at[window, k],
            send_sem=att_send.at[window, k],
            recv_sem=att_recv.at[window, k],
            device_id=at_seq(k),
            device_id_type=MESH,
        )

    w_copies = []

    def w_copy(src, dst, device):
        n = len(w_copies)
        copy = pltpu.make_async_remote_copy(
            src_ref=src,
            dst_ref=dst,
            send_sem=w_send.at[n],
            recv_sem=w_recv.at[n],
            device_id=device,
            device_id_type=MESH,
        )
        w_copies.append(copy)
        return copy

    def slot_rows(slot, start, count):
        if slot == 0:
            return wout_ref.at[pl.ds(start, count), :]
        return wall.at[slot, pl.ds(start, count), :]

    share_member, share_win = share_levels(members, blocks, head_width)
    part = head_width // (1 + share_member) // (1 + share_win)
    pair = part * (1 + share_member)
    w_stages = [[]]
    held = [0]
    masks = [1 << b for b in reversed(range(bits))]
    for mask in masks:
        grown = [k | mask for k in held]
        if mask == 1:
            direct = [w_copy(slot_rows(0, 0, head_width), wall.at[1], at_seq(1))]
            w_stages[0] += direct
            w_stages.append(
                [w_copy(wall.at[k], wall.at[k | 1], at_seq(1)) for k in held if k]
            )
        else:
            start = 0
            if share_win:
                start = (win % 2) * pair
            own = start
            if share_member:
                own = start + member * part
            own = pl.multiple_of(own, 16) if share_win or share_member else own
            stage = [
                w_copy(slot_rows(k, own, part), wall.at[k | mask, pl.ds(own, part), :], at_seq(mask))
                for k in held
            ]
            if held == [0]:
                w_stages[0] += stage
            else:
                w_stages.append(stage)
            if share_member:
                w_stages.append(
                    [
                        w_copy(
                            wall.at[k, pl.ds(own, part), :],
                            wall.at[k, pl.ds(own, part), :],
                            {"member": flip(member)},
                        )
                        for k in grown
                    ]
                )
            if share_win:
                begin = pl.multiple_of(start, 16)
                w_stages.append(
                    [
                        w_copy(
                            wall.at[k, pl.ds(begin, pair), :],
                            wall.at[k, pl.ds(begin, pair), :],
                            {"win": flip(win)},
                        )
                        for k in grown
                    ]
                )
        held = held + grown

    def w_stage(n):
        if 0 < n <= len(w_stages):
            for copy in w_stages[n - 1]:
                copy.wait_recv()
        if n < len(w_stages):
            for copy in w_stages[n]:
                copy.start()

    def norm(i):
        pltpu.make_async_copy(pix.at[i], pix.at[i], fetch_recv.at[i]).wait()
        gain = gain_ref[...]
        offset = bias_ref[...]
        for a in range(step):
            values = pix[i, a].astype(jnp.float32)
            average = jnp.mean(values, axis=-1, keepdims=True)
            centred = values - average
            variance = jnp.mean(centred * centred, axis=-1, keepdims=True)
            scaled = centred * lax.rsqrt(variance + 1e-05) * gain + offset
            nrm[0, i, a] = scaled.astype(jnp.bfloat16)

    def send(i):
        for slot in children(0, lanes):
            gather_copy(slot, i).start()

    inner = [k for k in range(1, lanes) if children(k, lanes)]
    inner.sort(key=lambda k: (bin(k).count("1"), -k))

    def forward(i):
        for k in inner:
            gather_copy(k, i).wait_recv()
            for slot in children(k, lanes):
                gather_copy(slot, i).start()

    def project_qkv(i):
        for k in range(1, lanes):
            if not children(k, lanes):
                gather_copy(k, i).wait_recv()
        window, place = i // 4, i % 4
        x = nrm[:, i].reshape(lanes * group, width)
        lane = lax.broadcasted_iota(jnp.int32, (lanes * group, PADDED), 1)
        ones = jnp.where(lane == CHANNEL_PER_PART, 1.0, 0.0).astype(jnp.bfloat16)
        q_extra = extq[i].reshape(lanes * group, PADDED)
        k_extra = extk[i].reshape(lanes * group, PADDED)
        for t, extra in enumerate((q_extra, k_extra, ones)):
            y = jnp.dot(x, wpad[t], preferred_element_type=jnp.float32).astype(jnp.bfloat16)
            for h in range(heads):
                part_y = y[:, h * PADDED : (h + 1) * PADDED] + extra
                qkv[t, window, :, place, :, h * PADDED : (h + 1) * PADDED] = part_y.reshape(
                    lanes, group, PADDED
                )

    def attend(window, k):
        for h in range(heads):
            span = slice(h * PADDED, (h + 1) * PADDED)
            tempered = scale_ref[h] * (LOG2E / math.sqrt(CHANNEL_PER_PART))
            q = qkv[0, window, k, :, :, span].reshape(chunk, PADDED)
            keys = qkv[1, window, :, :, :, span].reshape(lanes * chunk, PADDED)
            values = qkv[2, window, :, :, :, span].reshape(lanes * chunk, PADDED)
            scores = lax.dot_general(
                q, keys, (((1,), (1,)), ((), ())), preferred_element_type=jnp.float32
            )
            row_max = jnp.max(scores, axis=-1, keepdims=True)
            numerators = jnp.exp2((scores - row_max) * tempered).astype(jnp.bfloat16)
            summed = jnp.dot(numerators, values, preferred_element_type=jnp.float32)
            attended = summed / summed[:, CHANNEL_PER_PART : CHANNEL_PER_PART + 1]
            att_out[window, k, :, h * CHANNEL_PER_PART : (h + 1) * CHANNEL_PER_PART] = attended[
                :, :CHANNEL_PER_PART
            ].astype(jnp.bfloat16)

    def attend_and_send(window, k):
        attend(window, k)

        @pl.when(k > 0)
        def _():
            attended_copy(window, k).start()

    tile = 512 if width % 512 == 0 else width

    def emit(window):
        for piece in range(4):
            i = window * 4 + piece
            first = window * WS + (piece % 2) * HALF
            yield pltpu.make_async_copy(
                obuf.at[i],
                out_ref.at[0, pl.ds((piece // 2) * step, step), 0, pl.ds(first, HALF), :],
                out_sem.at[i],
            )

    def residual(window, columns):
        return pix[window * 4 : window * 4 + 4, :, :, columns].reshape(chunk, tile).astype(jnp.float32)

    def project_out(window, ready, late):
        for start in range(0, width, tile):
            columns = slice(start, start + tile)
            total = residual(window, columns)
            for k in ready:
                source_ref = att_out if k == 0 else att_in
                total += jnp.dot(
                    source_ref[window, k], wall[k, :, columns], preferred_element_type=jnp.float32
                )
            if late:
                acc[:, columns] = total
            else:
                obuf[window * 4 : window * 4 + 4, :, :, columns] = total.astype(
                    jnp.bfloat16
                ).reshape(4, step, HALF, tile)
        for n, k in enumerate(late):
            attended_copy(window, k).wait_recv()
            for start in range(0, width, tile):
                columns = slice(start, start + tile)
                total = acc[:, columns] + jnp.dot(
                    att_in[window, k], wall[k, :, columns], preferred_element_type=jnp.float32
                )
                if n + 1 < len(late):
                    acc[:, columns] = total
                else:
                    obuf[window * 4 : window * 4 + 4, :, :, columns] = total.astype(
                        jnp.bfloat16
                    ).reshape(4, step, HALF, tile)
        for copy in emit(window):
            copy.start()

    barrier = pltpu.get_barrier_semaphore()
    greeted = [at_seq(k) for k in range(1, lanes)]
    greeted += [{"win": flip(win)}, {"win": (win + 2) % blocks}, {"win": (flip(win) + 2) % blocks}]
    if share_member:
        greeted.append({"member": flip(member)})
    for device in greeted:
        pl.semaphore_signal(barrier, inc=1, device_id=device, device_id_type=MESH)
    for copy in locals_:
        copy.start()
    raw_copy = pltpu.make_async_copy(wqkv_ref, raw, local_sem.at[0])
    raw_copy.start()
    own_copy = pltpu.make_async_copy(wout_ref, wall.at[0], local_sem.at[1])
    own_copy.start()
    pl.semaphore_wait(barrier, len(greeted))
    for copy in fetches:
        copy.start()
    w_stage(0)

    @pl.loop(0, 2)
    def _(i):
        norm(i)
        send(i)

    labt[...] = jnp.zeros_like(labt)
    for k in range(lanes):
        lane_of = xor(me, k, bits)
        for a in range(rows):
            labt[a : a + 1, :cols] = label_ref[0, pl.ds(a * lanes + lane_of, 1), :].astype(jnp.float32)
        turned = jnp.transpose(labt[...])
        for i in range(pieces):
            first = (i // 4) * WS + (i % 2) * HALF
            for a in range(step):
                row = ((i // 2) % 2) * step + a
                label = turned[first : first + HALF, row : row + 1].astype(jnp.int32)
                lane = lax.broadcasted_iota(jnp.int32, (HALF, PADDED), 1) - CHANNEL_PER_PART
                same = lane == label
                extq[i, k, a] = jnp.where(same, 1.0, 0.0).astype(jnp.bfloat16)
                extk[i, k, a] = jnp.where(
                    jnp.logical_and(lane >= 0, jnp.logical_not(same)), -1e30, 0.0
                ).astype(jnp.bfloat16)

    raw_copy.wait()
    tall = width // 4

    @pl.loop(0, 12)
    def _(n):
        t, r = n // 4, pl.multiple_of((n % 4) * tall, tall)
        for h in range(heads):
            part_w = raw[t, pl.ds(r, tall), h * CHANNEL_PER_PART : (h + 1) * CHANNEL_PER_PART]
            empty = jnp.zeros((tall, PADDED - CHANNEL_PER_PART), part_w.dtype)
            wpad[t, pl.ds(r, tall), h * PADDED : (h + 1) * PADDED] = jnp.concatenate(
                [part_w, empty], axis=1
            )

    @pl.loop(2, 4)
    def _(i):
        norm(i)
        send(i)

    w_stage(1)

    @pl.loop(0, 4)
    def _(i):
        norm(i + 4)
        send(i + 4)
        forward(i)

        @pl.when(i > 0)
        def _():
            project_qkv(i - 1)

        @pl.when(i == 2)
        def _():
            w_stage(2)

    per = lanes // 4

    @pl.loop(0, 4)
    def _(i):
        forward(i + 4)
        project_qkv(i + 3)
        for n in range(per):
            attend_and_send(0, lanes - 1 - i * per - n)

    for n in range(3, len(w_stages)):
        w_stage(n)
    project_qkv(pieces - 1)

    @pl.loop(0, lanes)
    def _(i):
        attend_and_send(1, lanes - 1 - i)

    for n in range(max(3, len(w_stages)), len(w_stages) + 1):
        w_stage(n)
    own_copy.wait()
    for k in reversed(range(1, lanes)):
        attended_copy(0, k).wait_recv()
    project_out(0, list(range(lanes)), [])
    for window in range(1, window_count):
        project_out(window, [0], [1] + list(reversed(range(2, lanes))))

    for copy in fetches:
        copy.wait_send()

    @pl.loop(0, pieces)
    def _(i):
        for k in range(1, lanes):
            gather_copy(k, i).wait_send()

    for copy in w_copies:
        copy.wait_send()
    for window in range(window_count):
        for k in range(1, lanes):
            attended_copy(window, k).wait_send()
        for copy in emit(window):
            copy.wait()


def share_levels(members, blocks, head_width):
    by_member = int(members == 2 and head_width % 32 == 0)
    by_win = int(by_member and blocks % 2 == 0 and head_width % 64 == 0)
    return by_member, by_win


def on_device(x, labels, gain, offset, wqkv, scale, wout):
    lanes = lax.axis_size("seq")
    blocks = lax.axis_size("win")
    members = lax.axis_size("member")
    _, rows, _, cols, width = x.shape
    step = rows // 2
    window_count = cols // WS
    pieces = 4 * window_count
    head_width = wout.shape[0]
    heads = head_width // CHANNEL_PER_PART
    group = step * HALF
    chunk = 4 * group
    half = jnp.bfloat16
    w_count = 4 * lanes
    vmem = pl.BlockSpec(memory_space=pltpu.VMEM)
    anywhere = pl.BlockSpec(memory_space=pl.ANY)
    return pl.pallas_call(
        functools.partial(layer_kernel, lanes, blocks, members),
        out_shape=jax.ShapeDtypeStruct(x.shape, x.dtype),
        in_specs=[
            pl.BlockSpec(memory_space=pltpu.SMEM),
            anywhere,
            vmem,
            vmem,
            vmem,
            anywhere,
            anywhere,
        ],
        out_specs=anywhere,
        scratch_shapes=[
            pltpu.VMEM((pieces, step, HALF, width), half),
            pltpu.VMEM((lanes, pieces, step, HALF, width), half),
            pltpu.VMEM(wqkv.shape, half),
            pltpu.VMEM((3, width, heads * PADDED), half),
            pltpu.VMEM((lanes, head_width, width), half),
            pltpu.VMEM((3, window_count, lanes, 4, group, heads * PADDED), half),
            pltpu.VMEM((pieces, lanes, step, HALF, PADDED), half),
            pltpu.VMEM((pieces, lanes, step, HALF, PADDED), half),
            pltpu.VMEM((8, 128), jnp.float32),
            pltpu.VMEM((window_count, lanes, chunk, head_width), half),
            pltpu.VMEM((window_count, lanes, chunk, head_width), half),
            pltpu.VMEM((chunk, width), jnp.float32),
            pltpu.VMEM((pieces, step, HALF, width), half),
            pltpu.SemaphoreType.DMA((pieces,)),
            pltpu.SemaphoreType.DMA((pieces,)),
            pltpu.SemaphoreType.DMA((lanes, pieces)),
            pltpu.SemaphoreType.DMA((lanes, pieces)),
            pltpu.SemaphoreType.DMA((window_count, lanes)),
            pltpu.SemaphoreType.DMA((window_count, lanes)),
            pltpu.SemaphoreType.DMA((w_count,)),
            pltpu.SemaphoreType.DMA((w_count,)),
            pltpu.SemaphoreType.DMA((2,)),
            pltpu.SemaphoreType.DMA((pieces,)),
        ],
        compiler_params=pltpu.CompilerParams(
            collective_id=0, has_side_effects=True, vmem_limit_bytes=58 << 20
        ),
    )(scale, x, labels, gain, offset, wqkv, wout)


def solution(mesh):
    in_specs = (
        P(("member", "win"), None, "seq", None, None),
        P(("member", "win"), None, None),
        P(),
        P(),
        P(None, None, "seq"),
        P("seq"),
        P("seq", None),
    )
    out_specs = P(("member", "win"), None, "seq", None, None)
    return jax.shard_map(
        on_device, mesh=mesh, in_specs=in_specs, out_specs=out_specs, check_vma=False
    )
```

profile of v0, /device:TPU:0, one launch (start us, length us, event | category | flops | bytes accessed | tf_op | source)
XLA Modules:
  0.0 71.5 jit_solution(4531709900512655386)
XLA Ops:
  0.0 68.8 %shard_map.73 = bf16[1,8,1,64,1536]{4,3,2,1,0:T(8,128)(2,1)} custom-call(f32[4]{0:T(128)} %scale_ref.1, bf16[1,8,1,64,1536]{4,3,2,1,0:T(8,128)(2,1)} %x_ref.1, s32[1,32,64]{2,1,0:T(8,128)} %label_ref.1, f32[1536]{0:T(1024)} %gain_ref.1, f32[1536]{0:T(1024)} %bias_ref.1, bf16[3,1536,384]{2,1,0:T(8,128)(2,1)} %wqkv_ref.1, bf16[384,1536]{1,0:T(8,128)(2,1)} %wout_ref.1), custom_call_target="tpu_custom_call" | custom-call | tf_op jit(solution)/shard_map/pallas_call | solution.py:475
  68.8 2.7 %copy.9 = bf16[1,8,1,64,1536]{4,3,2,1,0:T(8,128)(2,1)} copy(bf16[1,8,1,64,1536]{4,3,2,1,0:T(8,128)(2,1)} %shard_map.73) | data formatting | bytes 3145728
where the time goes:
time: 71.7 us; the launch traced here: 71.5 us
  Pallas kernels  68.8 us (96%)
  local copies, waits for them, and re-layouts  2.65 us (4%)
    pallas_call x1, Pallas kernels, on_device(): pl.pallas_call(functools.partial(layer_kernel, lanes, blocks, members), o...  68.8 us
    unnamed x1, local copies, waits for them, and re-layouts  2.65 us

commit v1 on v0

--- a/solution.py
+++ b/solution.py
@@ -23,8 +23,8 @@
     return value + mask - 2 * both
 
 
-def flip(value):
-    return value + 1 - 2 * (value % 2)
+def flip(value, bit=1):
+    return value + bit - 2 * bit * ((value // bit) % 2)
 
 
 def children(slot, lanes):
@@ -37,14 +37,18 @@
     lanes,
     blocks,
     members,
+    scale_hbm,
+    x_ref,
+    label_hbm,
+    gain_hbm,
+    bias_hbm,
+    wqkv_ref,
+    wout_ref,
+    out_ref,
     scale_ref,
-    x_ref,
     label_ref,
     gain_ref,
     bias_ref,
-    wqkv_ref,
-    wout_ref,
-    out_ref,
     pix,
     nrm,
     raw,
@@ -57,7 +61,6 @@
     att_out,
     att_in,
     acc,
-    obuf,
     fetch_send,
     fetch_recv,
     norm_send,
@@ -67,7 +70,6 @@
     w_send,
     w_recv,
     local_sem,
-    out_sem,
 ):
     me = lax.axis_index("seq")
     win = lax.axis_index("win")
@@ -264,7 +266,7 @@
     def attend(window, k):
         for h in range(heads):
             span = slice(h * PADDED, (h + 1) * PADDED)
-            tempered = scale_ref[h] * (LOG2E / math.sqrt(CHANNEL_PER_PART))
+            tempered = scale_ref[h : h + 1].reshape(1, 1) * (LOG2E / math.sqrt(CHANNEL_PER_PART))
             q = qkv[0, window, k, :, :, span].reshape(chunk, PADDED)
             keys = qkv[1, window, :, :, :, span].reshape(lanes * chunk, PADDED)
             values = qkv[2, window, :, :, :, span].reshape(lanes * chunk, PADDED)
@@ -288,15 +290,12 @@
 
     tile = 512 if width % 512 == 0 else width
 
-    def emit(window):
+    def store(window, columns, total):
+        total = total.astype(jnp.bfloat16).reshape(4, step, HALF, tile)
         for piece in range(4):
-            i = window * 4 + piece
             first = window * WS + (piece % 2) * HALF
-            yield pltpu.make_async_copy(
-                obuf.at[i],
-                out_ref.at[0, pl.ds((piece // 2) * step, step), 0, pl.ds(first, HALF), :],
-                out_sem.at[i],
-            )
+            start = (piece // 2) * step
+            out_ref[0, start : start + step, 0, first : first + HALF, columns] = total[piece]
 
     def residual(window, columns):
         return pix[window * 4 : window * 4 + 4, :, :, columns].reshape(chunk, tile).astype(jnp.float32)
@@ -313,9 +312,7 @@
             if late:
                 acc[:, columns] = total
             else:
-                obuf[window * 4 : window * 4 + 4, :, :, columns] = total.astype(
-                    jnp.bfloat16
-                ).reshape(4, step, HALF, tile)
+                store(window, columns, total)
         for n, k in enumerate(late):
             attended_copy(window, k).wait_recv()
             for start in range(0, width, tile):
@@ -326,11 +323,7 @@
                 if n + 1 < len(late):
                     acc[:, columns] = total
                 else:
-                    obuf[window * 4 : window * 4 + 4, :, :, columns] = total.astype(
-                        jnp.bfloat16
-                    ).reshape(4, step, HALF, tile)
-        for copy in emit(window):
-            copy.start()
+                    store(window, columns, total)
 
     barrier = pltpu.get_barrier_semaphore()
     greeted = [at_seq(k) for k in range(1, lanes)]
@@ -341,14 +334,27 @@
         pl.semaphore_signal(barrier, inc=1, device_id=device, device_id_type=MESH)
     for copy in locals_:
         copy.start()
-    raw_copy = pltpu.make_async_copy(wqkv_ref, raw, local_sem.at[0])
-    raw_copy.start()
-    own_copy = pltpu.make_async_copy(wout_ref, wall.at[0], local_sem.at[1])
-    own_copy.start()
+    loads = [
+        pltpu.make_async_copy(src, dst, local_sem.at[n])
+        for n, (src, dst) in enumerate(
+            [
+                (gain_hbm, gain_ref),
+                (bias_hbm, bias_ref),
+                (label_hbm, label_ref),
+                (scale_hbm, scale_ref),
+                (wqkv_ref, raw),
+                (wout_ref, wall.at[0]),
+            ]
+        )
+    ]
+    for copy in loads:
+        copy.start()
     pl.semaphore_wait(barrier, len(greeted))
     for copy in fetches:
         copy.start()
     w_stage(0)
+    loads[0].wait()
+    loads[1].wait()
 
     @pl.loop(0, 2)
     def _(i):
@@ -356,6 +362,7 @@
         send(i)
 
     labt[...] = jnp.zeros_like(labt)
+    loads[2].wait()
     for k in range(lanes):
         lane_of = xor(me, k, bits)
         for a in range(rows):
@@ -373,7 +380,8 @@
                     jnp.logical_and(lane >= 0, jnp.logical_not(same)), -1e30, 0.0
                 ).astype(jnp.bfloat16)
 
-    raw_copy.wait()
+    loads[3].wait()
+    loads[4].wait()
     tall = width // 4
 
     @pl.loop(0, 12)
@@ -426,7 +434,7 @@
 
     for n in range(max(3, len(w_stages)), len(w_stages) + 1):
         w_stage(n)
-    own_copy.wait()
+    loads[5].wait()
     for k in reversed(range(1, lanes)):
         attended_copy(0, k).wait_recv()
     project_out(0, list(range(lanes)), [])
@@ -446,8 +454,6 @@
     for window in range(window_count):
         for k in range(1, lanes):
             attended_copy(window, k).wait_send()
-        for copy in emit(window):
-            copy.wait()
 
 
 def share_levels(members, blocks, head_width):
@@ -470,22 +476,18 @@
     chunk = 4 * group
     half = jnp.bfloat16
     w_count = 4 * lanes
-    vmem = pl.BlockSpec(memory_space=pltpu.VMEM)
-    anywhere = pl.BlockSpec(memory_space=pl.ANY)
+    in_hbm = functools.partial(pltpu.with_memory_space_constraint, memory_space=pltpu.HBM)
+    operands = (scale, x, labels, gain, offset, wqkv, wout)
     return pl.pallas_call(
         functools.partial(layer_kernel, lanes, blocks, members),
-        out_shape=jax.ShapeDtypeStruct(x.shape, x.dtype),
-        in_specs=[
-            pl.BlockSpec(memory_space=pltpu.SMEM),
-            anywhere,
-            vmem,
-            vmem,
-            vmem,
-            anywhere,
-            anywhere,
-        ],
-        out_specs=anywhere,
+        out_shape=pltpu.VMEM(x.shape, x.dtype),
+        in_specs=[pl.BlockSpec(memory_space=pltpu.HBM)] * 7,
+        out_specs=pl.BlockSpec(memory_space=pltpu.VMEM),
         scratch_shapes=[
+            pltpu.VMEM(scale.shape, scale.dtype),
+            pltpu.VMEM(labels.shape, labels.dtype),
+            pltpu.VMEM(gain.shape, gain.dtype),
+            pltpu.VMEM(offset.shape, offset.dtype),
             pltpu.VMEM((pieces, step, HALF, width), half),
             pltpu.VMEM((lanes, pieces, step, HALF, width), half),
             pltpu.VMEM(wqkv.shape, half),
@@ -498,7 +500,6 @@
             pltpu.VMEM((window_count, lanes, chunk, head_width), half),
             pltpu.VMEM((window_count, lanes, chunk, head_width), half),
             pltpu.VMEM((chunk, width), jnp.float32),
-            pltpu.VMEM((pieces, step, HALF, width), half),
             pltpu.SemaphoreType.DMA((pieces,)),
             pltpu.SemaphoreType.DMA((pieces,)),
             pltpu.SemaphoreType.DMA((lanes, pieces)),
@@ -507,13 +508,12 @@
             pltpu.SemaphoreType.DMA((window_count, lanes)),
             pltpu.SemaphoreType.DMA((w_count,)),
             pltpu.SemaphoreType.DMA((w_count,)),
-            pltpu.SemaphoreType.DMA((2,)),
-            pltpu.SemaphoreType.DMA((pieces,)),
+            pltpu.SemaphoreType.DMA((6,)),
         ],
         compiler_params=pltpu.CompilerParams(
-            collective_id=0, has_side_effects=True, vmem_limit_bytes=58 << 20
+            collective_id=0, has_side_effects=True, vmem_limit_bytes=42 << 20
         ),
-    )(scale, x, labels, gain, offset, wqkv, wout)
+    )(*[in_hbm(o) if o.size > 1 else o for o in operands])
 
 
 def solution(mesh):

time: 71.7 us -> 68.4 us (0.954)
  Pallas kernels: 68.8 us -> 67.1 us
  local copies, waits for them, and re-layouts: 2.65 us -> 1.15 us
    pallas_call x1, Pallas kernels: 68.8 us -> 67.1 us  [on_device(): pl.pallas_call(functools.partial(layer_kernel, lanes, blocks, members), o...]
    unnamed x1, local copies, waits for them, and re-layouts: 2.65 us -> 1.15 us
where the time goes in v1:
time: 68.4 us; the launch traced here: 68.2 us
  Pallas kernels  67.1 us (98%)
  local copies, waits for them, and re-layouts  1.15 us (2%)
    pallas_call x1, Pallas kernels, on_device(): pl.pallas_call(functools.partial(layer_kernel, lanes, blocks, members), o...  67.1 us

profile of v1, /device:TPU:0, one launch (start us, length us, event | category | flops | bytes accessed | tf_op | source)
XLA Modules:
  0.0 68.2 jit_solution(8884523529042017230)
XLA Ops:
  0.0 67.1 %shard_map.73 = bf16[1,8,1,64,1536]{4,3,2,1,0:T(8,128)(2,1)S(1)} custom-call(f32[4]{0:T(128)} %scale_hbm.1, bf16[1,8,1,64,1536]{4,3,2,1,0:T(8,128)(2,1)} %x_ref.1, s32[1,32,64]{2,1,0:T(8,128)} %label_hbm.1, f32[1536]{0:T(1024)} %gain_hbm.1, f32[1536]{0:T(1024)} %bias_hbm.1, bf16[3,1536,384]{2,1,0:T(8,128)(2,1)} %wqkv_ref.1, bf16[384,1536]{1,0:T(8,128)(2,1)} %wout_ref.1), custom_call_target="tpu_custom_call" | custom-call | tf_op jit(solution)/shard_map/pallas_call | solution.py:481
  67.1 1.1 %copy.9 = bf16[1,8,1,64,1536]{4,3,2,1,0:T(8,128)(2,1)} copy(bf16[1,8,1,64,1536]{4,3,2,1,0:T(8,128)(2,1)S(1)} %shard_map.73) | data formatting | bytes 3145728

commit v2 on v1

--- a/solution.py
+++ b/solution.py
@@ -70,6 +70,7 @@
     w_send,
     w_recv,
     local_sem,
+    known_sem,
 ):
     me = lax.axis_index("seq")
     win = lax.axis_index("win")
@@ -95,26 +96,28 @@
 
     west = (win + blocks - 2) % blocks
     fetches = []
+    corners = []
     locals_ = []
+
+    def fetch_copy(src, dst, n, to):
+        return pltpu.make_async_remote_copy(
+            src_ref=src,
+            dst_ref=dst,
+            send_sem=fetch_send.at[n],
+            recv_sem=fetch_recv.at[n],
+            device_id={"win": to},
+            device_id_type=MESH,
+        )
+
     for i in range(pieces):
         place, first, src = source(i)
         if place == 0 and first < cols:
             locals_.append(pltpu.make_async_copy(src, pix.at[i], fetch_recv.at[i]))
             continue
-        if first < cols:
-            to = flip(win)
+        if place == 1 and first >= cols:
+            corners.append(fetch_copy(src, pix.at[i], i, flip(west)))
         else:
-            to = west if place == 0 else flip(west)
-        fetches.append(
-            pltpu.make_async_remote_copy(
-                src_ref=src,
-                dst_ref=pix.at[i],
-                send_sem=fetch_send.at[i],
-                recv_sem=fetch_recv.at[i],
-                device_id={"win": to},
-                device_id_type=MESH,
-            )
-        )
+            fetches.append(fetch_copy(src, pix.at[i], i, flip(win) if place else west))
 
     def gather_copy(slot, i):
         parent = slot & (slot - 1)
@@ -157,67 +160,74 @@
             return wout_ref.at[pl.ds(start, count), :]
         return wall.at[slot, pl.ds(start, count), :]
 
-    share_member, share_win = share_levels(members, blocks, head_width)
-    part = head_width // (1 + share_member) // (1 + share_win)
-    pair = part * (1 + share_member)
-    w_stages = [[]]
+    share_member, share_win, share_far = share_levels(members, blocks, head_width)
+    part = head_width // (1 + share_member) // (1 + share_win) // (1 + share_far)
+    near, far = (win % 2) * share_win, ((win // 2) % 2) * share_far
+    mine = member * share_member
+
+    def rows_of(b, a, m, count=1):
+        start = (((b * (1 + share_far)) + a) * (1 + share_member) + m) * part
+        if not isinstance(start, int):
+            start = pl.multiple_of(start, 16)
+        return start, count * part
+
+    def relay(slots, place, device):
+        return [
+            w_copy(wall.at[k, pl.ds(*place), :], wall.at[k, pl.ds(*place), :], device)
+            for k in slots
+        ]
+
+    w_stages = []
     held = [0]
-    masks = [1 << b for b in reversed(range(bits))]
-    for mask in masks:
+    pending = []
+    for mask in [1 << b for b in reversed(range(bits))]:
         grown = [k | mask for k in held]
         if mask == 1:
             direct = [w_copy(slot_rows(0, 0, head_width), wall.at[1], at_seq(1))]
-            w_stages[0] += direct
-            w_stages.append(
-                [w_copy(wall.at[k], wall.at[k | 1], at_seq(1)) for k in held if k]
-            )
+            last = [w_copy(wall.at[k], wall.at[k | 1], at_seq(1)) for k in held if k]
+            if w_stages:
+                w_stages[0] = (w_stages[0][0], w_stages[0][1] + direct)
+                w_stages.append((pending, last))
+            else:
+                w_stages.append(([], direct))
+            pending = last + direct
         else:
-            start = 0
-            if share_win:
-                start = (win % 2) * pair
-            own = start
-            if share_member:
-                own = start + member * part
-            own = pl.multiple_of(own, 16) if share_win or share_member else own
+            place = rows_of(near, far, mine)
             stage = [
-                w_copy(slot_rows(k, own, part), wall.at[k | mask, pl.ds(own, part), :], at_seq(mask))
+                w_copy(slot_rows(k, *place), wall.at[k | mask, pl.ds(*place), :], at_seq(mask))
                 for k in held
             ]
-            if held == [0]:
-                w_stages[0] += stage
+            w_stages.append((pending, stage))
+            pending = stage
+            if share_far:
+                other = 1 - far
+                up = relay(grown, place, {"member": flip(member)})
+                over = relay(grown, place, {"win": flip(win, 2)})
+                w_stages.append((pending, up + over))
+                across = relay(grown, rows_of(near, other, mine), {"member": flip(member)})
+                batch = relay(grown, rows_of(near, far, 0, 2), {"win": flip(win)})
+                batch += relay(grown, rows_of(near, other, mine), {"win": flip(win)})
+                w_stages.append((up + over, across + batch))
+                rest = relay(grown, rows_of(near, other, 1 - mine), {"win": flip(win)})
+                w_stages.append((across, rest))
+                pending = batch + rest
             else:
-                w_stages.append(stage)
-            if share_member:
-                w_stages.append(
-                    [
-                        w_copy(
-                            wall.at[k, pl.ds(own, part), :],
-                            wall.at[k, pl.ds(own, part), :],
-                            {"member": flip(member)},
-                        )
-                        for k in grown
-                    ]
-                )
-            if share_win:
-                begin = pl.multiple_of(start, 16)
-                w_stages.append(
-                    [
-                        w_copy(
-                            wall.at[k, pl.ds(begin, pair), :],
-                            wall.at[k, pl.ds(begin, pair), :],
-                            {"win": flip(win)},
-                        )
-                        for k in grown
-                    ]
-                )
+                if share_member:
+                    stage = relay(grown, place, {"member": flip(member)})
+                    w_stages.append((pending, stage))
+                    pending = stage
+                if share_win:
+                    stage = relay(grown, rows_of(near, 0, 0, 1 + share_member), {"win": flip(win)})
+                    w_stages.append((pending, stage))
+                    pending = stage
         held = held + grown
+    w_stages.append((pending, []))
 
     def w_stage(n):
-        if 0 < n <= len(w_stages):
-            for copy in w_stages[n - 1]:
+        if n < len(w_stages):
+            for copy in w_stages[n][0]:
                 copy.wait_recv()
-        if n < len(w_stages):
-            for copy in w_stages[n]:
+            for copy in w_stages[n][1]:
                 copy.start()
 
     def norm(i):
@@ -263,15 +273,21 @@
                     lanes, group, PADDED
                 )
 
+    def scores_of(window, k, h):
+        span = slice(h * PADDED, (h + 1) * PADDED)
+        q = qkv[0, window, k, :, :, span].reshape(chunk, PADDED)
+        keys = qkv[1, window, :, :, :, span].reshape(lanes * chunk, PADDED)
+        return lax.dot_general(
+            q, keys, (((1,), (1,)), ((), ())), preferred_element_type=jnp.float32
+        )
+
     def attend(window, k):
+        scores = scores_of(window, k, 0)
         for h in range(heads):
-            span = slice(h * PADDED, (h + 1) * PADDED)
+            following = scores_of(window, k, h + 1) if h + 1 < heads else None
             tempered = scale_ref[h : h + 1].reshape(1, 1) * (LOG2E / math.sqrt(CHANNEL_PER_PART))
-            q = qkv[0, window, k, :, :, span].reshape(chunk, PADDED)
-            keys = qkv[1, window, :, :, :, span].reshape(lanes * chunk, PADDED)
-            values = qkv[2, window, :, :, :, span].reshape(lanes * chunk, PADDED)
-            scores = lax.dot_general(
-                q, keys, (((1,), (1,)), ((), ())), preferred_element_type=jnp.float32
+            values = qkv[2, window, :, :, :, h * PADDED : (h + 1) * PADDED].reshape(
+                lanes * chunk, PADDED
             )
             row_max = jnp.max(scores, axis=-1, keepdims=True)
             numerators = jnp.exp2((scores - row_max) * tempered).astype(jnp.bfloat16)
@@ -280,6 +296,7 @@
             att_out[window, k, :, h * CHANNEL_PER_PART : (h + 1) * CHANNEL_PER_PART] = attended[
                 :, :CHANNEL_PER_PART
             ].astype(jnp.bfloat16)
+            scores = following
 
     def attend_and_send(window, k):
         attend(window, k)
@@ -327,7 +344,9 @@
 
     barrier = pltpu.get_barrier_semaphore()
     greeted = [at_seq(k) for k in range(1, lanes)]
-    greeted += [{"win": flip(win)}, {"win": (win + 2) % blocks}, {"win": (flip(win) + 2) % blocks}]
+    greeted += [{"win": flip(win)}, {"win": (win + 2) % blocks}]
+    if share_far and blocks != 4:
+        greeted.append({"win": flip(win, 2)})
     if share_member:
         greeted.append({"member": flip(member)})
     for device in greeted:
@@ -350,6 +369,9 @@
     for copy in loads:
         copy.start()
     pl.semaphore_wait(barrier, len(greeted))
+    pl.semaphore_signal(
+        known_sem, inc=1, device_id={"win": (win + 2) % blocks}, device_id_type=MESH
+    )
     for copy in fetches:
         copy.start()
     w_stage(0)
@@ -360,6 +382,10 @@
     def _(i):
         norm(i)
         send(i)
+
+    pl.semaphore_wait(known_sem, 1)
+    for copy in corners:
+        copy.start()
 
     labt[...] = jnp.zeros_like(labt)
     loads[2].wait()
@@ -411,29 +437,41 @@
         def _():
             project_qkv(i - 1)
 
+    per = lanes // 4
+
+    @pl.loop(0, 4)
+    def _(i):
+        forward(i + 4)
+        project_qkv(i + 3)
+
+        @pl.when(i == 0)
+        def _():
+            w_stage(2)
+
         @pl.when(i == 2)
         def _():
-            w_stage(2)
-
-    per = lanes // 4
-
-    @pl.loop(0, 4)
-    def _(i):
-        forward(i + 4)
-        project_qkv(i + 3)
-        for n in range(per):
-            attend_and_send(0, lanes - 1 - i * per - n)
-
-    for n in range(3, len(w_stages)):
+            w_stage(3)
+
+        @pl.when(i < 3)
+        def _():
+            for n in range(per):
+                attend_and_send(0, lanes - 1 - i * per - n)
+
+    project_qkv(pieces - 1)
+
+    @pl.loop(0, 2 * per)
+    def _(i):
+        attend_and_send(1, lanes - 1 - i)
+
+    for n in range(4, len(w_stages) - 1):
         w_stage(n)
-    project_qkv(pieces - 1)
-
-    @pl.loop(0, lanes)
-    def _(i):
-        attend_and_send(1, lanes - 1 - i)
-
-    for n in range(max(3, len(w_stages)), len(w_stages) + 1):
-        w_stage(n)
+
+    @pl.loop(0, 3 * per)
+    def _(i):
+        window = (i + 2 * per) // (3 * per)
+        attend_and_send(window, per - 1 - i + 2 * per * window)
+
+    w_stage(max(4, len(w_stages) - 1))
     loads[5].wait()
     for k in reversed(range(1, lanes)):
         attended_copy(0, k).wait_recv()
@@ -441,7 +479,7 @@
     for window in range(1, window_count):
         project_out(window, [0], [1] + list(reversed(range(2, lanes))))
 
-    for copy in fetches:
+    for copy in fetches + corners:
         copy.wait_send()
 
     @pl.loop(0, pieces)
@@ -459,7 +497,8 @@
 def share_levels(members, blocks, head_width):
     by_member = int(members == 2 and head_width % 32 == 0)
     by_win = int(by_member and blocks % 2 == 0 and head_width % 64 == 0)
-    return by_member, by_win
+    by_far = int(by_win and blocks % 4 == 0 and head_width % 128 == 0)
+    return by_member, by_win, by_far
 
 
 def on_device(x, labels, gain, offset, wqkv, scale, wout):
@@ -509,6 +548,7 @@
             pltpu.SemaphoreType.DMA((w_count,)),
             pltpu.SemaphoreType.DMA((w_count,)),
             pltpu.SemaphoreType.DMA((6,)),
+            pltpu.SemaphoreType.REGULAR,
         ],
         compiler_params=pltpu.CompilerParams(
             collective_id=0, has_side_effects=True, vmem_limit_bytes=42 << 20

time: 68.4 us -> 63.2 us (0.924)
  Pallas kernels: 67.1 us -> 61.9 us
    pallas_call x1, Pallas kernels: 67.1 us -> 61.9 us  [on_device(): pl.pallas_call(functools.partial(layer_kernel, lanes, blocks, members), o...]
where the time goes in v2:
time: 63.2 us; the launch traced here: 63 us
  Pallas kernels  61.9 us (98%)
  local copies, waits for them, and re-layouts  1.15 us (2%)
    pallas_call x1, Pallas kernels, on_device(): pl.pallas_call(functools.partial(layer_kernel, lanes, blocks, members), o...  61.9 us

profile of v2, /device:TPU:0, one launch (start us, length us, event | category | flops | bytes accessed | tf_op | source)
XLA Modules:
  0.0 63.0 jit_solution(684030969875979632)
XLA Ops:
  0.0 61.9 %shard_map.73 = bf16[1,8,1,64,1536]{4,3,2,1,0:T(8,128)(2,1)S(1)} custom-call(f32[4]{0:T(128)} %scale_hbm.1, bf16[1,8,1,64,1536]{4,3,2,1,0:T(8,128)(2,1)} %x_ref.1, s32[1,32,64]{2,1,0:T(8,128)} %label_hbm.1, f32[1536]{0:T(1024)} %gain_hbm.1, f32[1536]{0:T(1024)} %bias_hbm.1, bf16[3,1536,384]{2,1,0:T(8,128)(2,1)} %wqkv_ref.1, bf16[384,1536]{1,0:T(8,128)(2,1)} %wout_ref.1), custom_call_target="tpu_custom_call" | custom-call | tf_op jit(solution)/shard_map/pallas_call | solution.py:520
  61.9 1.1 %copy.9 = bf16[1,8,1,64,1536]{4,3,2,1,0:T(8,128)(2,1)} copy(bf16[1,8,1,64,1536]{4,3,2,1,0:T(8,128)(2,1)S(1)} %shard_map.73) | data formatting | bytes 3145728

commit v3 on v2

--- a/solution.py
+++ b/solution.py
@@ -71,6 +71,7 @@
     w_recv,
     local_sem,
     known_sem,
+    near_sem,
 ):
     me = lax.axis_index("seq")
     win = lax.axis_index("win")
@@ -343,14 +344,23 @@
                     store(window, columns, total)
 
     barrier = pltpu.get_barrier_semaphore()
-    greeted = [at_seq(k) for k in range(1, lanes)]
-    greeted += [{"win": flip(win)}, {"win": (win + 2) % blocks}]
+    line = blocks == 4
+    greeted = [{"win": flip(win)}] if line else [{"win": (win + 2) % blocks}, {"win": flip(win)}]
+    greeted += [at_seq(k) for k in reversed(range(1, lanes))]
     if share_far and blocks != 4:
         greeted.append({"win": flip(win, 2)})
     if share_member:
         greeted.append({"member": flip(member)})
     for device in greeted:
         pl.semaphore_signal(barrier, inc=1, device_id=device, device_id_type=MESH)
+    if line:
+        beside = win + 2 * (win % 2) - 1
+        middle = ((win + 1) // 2) % 2
+
+        @pl.when(middle == 1)
+        def _():
+            pl.semaphore_signal(barrier, inc=1, device_id={"win": beside}, device_id_type=MESH)
+
     for copy in locals_:
         copy.start()
     loads = [
@@ -368,21 +378,34 @@
     ]
     for copy in loads:
         copy.start()
-    pl.semaphore_wait(barrier, len(greeted))
+    loads[0].wait()
+    loads[1].wait()
+
+    @pl.loop(0, 2)
+    def _(i):
+        norm(i)
+
+    pl.semaphore_wait(barrier, len(greeted) + (middle if line else 0))
+    send(0)
+    if line:
+
+        @pl.when(middle == 1)
+        def _():
+            for device in ({"win": beside}, {"win": flip(win)}):
+                pl.semaphore_signal(near_sem, inc=1, device_id=device, device_id_type=MESH)
+
+    for copy in fetches[:2]:
+        copy.start()
+    w_stage(0)
+    send(1)
+    if line:
+        pl.semaphore_wait(near_sem, 1)
     pl.semaphore_signal(
         known_sem, inc=1, device_id={"win": (win + 2) % blocks}, device_id_type=MESH
     )
-    for copy in fetches:
+    for copy in fetches[2:]:
         copy.start()
-    w_stage(0)
-    loads[0].wait()
-    loads[1].wait()
-
-    @pl.loop(0, 2)
-    def _(i):
-        norm(i)
-        send(i)
-
+    norm(4)
     pl.semaphore_wait(known_sem, 1)
     for copy in corners:
         copy.start()
@@ -429,7 +452,10 @@
 
     @pl.loop(0, 4)
     def _(i):
-        norm(i + 4)
+        @pl.when(i > 0)
+        def _():
+            norm(i + 4)
+
         send(i + 4)
         forward(i)
 
@@ -476,9 +502,6 @@
     for k in reversed(range(1, lanes)):
         attended_copy(0, k).wait_recv()
     project_out(0, list(range(lanes)), [])
-    for window in range(1, window_count):
-        project_out(window, [0], [1] + list(reversed(range(2, lanes))))
-
     for copy in fetches + corners:
         copy.wait_send()
 
@@ -489,7 +512,12 @@
 
     for copy in w_copies:
         copy.wait_send()
-    for window in range(window_count):
+    for k in range(1, lanes):
+        attended_copy(0, k).wait_send()
+    for window in range(1, window_count):
+        project_out(window, [0], [1] + list(reversed(range(2, lanes))))
+
+    for window in range(1, window_count):
         for k in range(1, lanes):
             attended_copy(window, k).wait_send()
 
@@ -549,6 +577,7 @@
             pltpu.SemaphoreType.DMA((w_count,)),
             pltpu.SemaphoreType.DMA((6,)),
             pltpu.SemaphoreType.REGULAR,
+            pltpu.SemaphoreType.REGULAR,
         ],
         compiler_params=pltpu.CompilerParams(
             collective_id=0, has_side_effects=True, vmem_limit_bytes=42 << 20

time: 63.2 us -> 62 us (0.981)
  Pallas kernels: 61.9 us -> 60.6 us
    pallas_call x1, Pallas kernels: 61.9 us -> 60.6 us  [on_device(): pl.pallas_call(functools.partial(layer_kernel, lanes, blocks, members), o...]
where the time goes in v3:
time: 62 us; the launch traced here: 61.8 us
  Pallas kernels  60.6 us (98%)
  local copies, waits for them, and re-layouts  1.15 us (2%)
    pallas_call x1, Pallas kernels, on_device(): pl.pallas_call(functools.partial(layer_kernel, lanes, blocks, members), o...  60.6 us

profile of v3, /device:TPU:0, one launch (start us, length us, event | category | flops | bytes accessed | tf_op | source)
XLA Modules:
  0.0 61.8 jit_solution(16522057525906569580)
XLA Ops:
  0.0 60.6 %shard_map.73 = bf16[1,8,1,64,1536]{4,3,2,1,0:T(8,128)(2,1)S(1)} custom-call(f32[4]{0:T(128)} %scale_hbm.1, bf16[1,8,1,64,1536]{4,3,2,1,0:T(8,128)(2,1)} %x_ref.1, s32[1,32,64]{2,1,0:T(8,128)} %label_hbm.1, f32[1536]{0:T(1024)} %gain_hbm.1, f32[1536]{0:T(1024)} %bias_hbm.1, bf16[3,1536,384]{2,1,0:T(8,128)(2,1)} %wqkv_ref.1, bf16[384,1536]{1,0:T(8,128)(2,1)} %wout_ref.1), custom_call_target="tpu_custom_call" | custom-call | tf_op jit(solution)/shard_map/pallas_call | solution.py:548
  60.6 1.1 %copy.9 = bf16[1,8,1,64,1536]{4,3,2,1,0:T(8,128)(2,1)} copy(bf16[1,8,1,64,1536]{4,3,2,1,0:T(8,128)(2,1)S(1)} %shard_map.73) | data formatting | bytes 3145728

commit v4 on v3

--- a/solution.py
+++ b/solution.py
@@ -131,12 +131,13 @@
             device_id_type=MESH,
         )
 
-    def attended_copy(window, k):
+    def attended_copy(window, k, side):
+        rows_sent = pl.ds(side * (chunk // 2), chunk // 2)
         return pltpu.make_async_remote_copy(
-            src_ref=att_out.at[window, k],
-            dst_ref=att_in.at[window, k],
-            send_sem=att_send.at[window, k],
-            recv_sem=att_recv.at[window, k],
+            src_ref=att_out.at[window, k, rows_sent, :],
+            dst_ref=att_in.at[window, k, rows_sent, :],
+            send_sem=att_send.at[window, k, side],
+            recv_sem=att_recv.at[window, k, side],
             device_id=at_seq(k),
             device_id_type=MESH,
         )
@@ -304,16 +305,18 @@
 
         @pl.when(k > 0)
         def _():
-            attended_copy(window, k).start()
+            for side in range(2):
+                attended_copy(window, k, side).start()
 
     tile = 512 if width % 512 == 0 else width
 
-    def store(window, columns, total):
-        total = total.astype(jnp.bfloat16).reshape(4, step, HALF, tile)
-        for piece in range(4):
+    def store(window, columns, total, begin=0):
+        count = total.shape[0] // group
+        total = total.astype(jnp.bfloat16).reshape(count, step, HALF, tile)
+        for piece in range(begin, begin + count):
             first = window * WS + (piece % 2) * HALF
             start = (piece // 2) * step
-            out_ref[0, start : start + step, 0, first : first + HALF, columns] = total[piece]
+            out_ref[0, start : start + step, 0, first : first + HALF, columns] = total[piece - begin]
 
     def residual(window, columns):
         return pix[window * 4 : window * 4 + 4, :, :, columns].reshape(chunk, tile).astype(jnp.float32)
@@ -331,17 +334,18 @@
                 acc[:, columns] = total
             else:
                 store(window, columns, total)
-        for n, k in enumerate(late):
-            attended_copy(window, k).wait_recv()
+        for n, (k, side) in enumerate([(k, side) for k in late for side in range(2)]):
+            attended_copy(window, k, side).wait_recv()
+            span = slice(side * (chunk // 2), (side + 1) * (chunk // 2))
             for start in range(0, width, tile):
                 columns = slice(start, start + tile)
-                total = acc[:, columns] + jnp.dot(
-                    att_in[window, k], wall[k, :, columns], preferred_element_type=jnp.float32
+                total = acc[span, columns] + jnp.dot(
+                    att_in[window, k, span, :], wall[k, :, columns], preferred_element_type=jnp.float32
                 )
-                if n + 1 < len(late):
-                    acc[:, columns] = total
+                if k != late[-1]:
+                    acc[span, columns] = total
                 else:
-                    store(window, columns, total)
+                    store(window, columns, total, 2 * side)
 
     barrier = pltpu.get_barrier_semaphore()
     line = blocks == 4
@@ -500,7 +504,8 @@
     w_stage(max(4, len(w_stages) - 1))
     loads[5].wait()
     for k in reversed(range(1, lanes)):
-        attended_copy(0, k).wait_recv()
+        for side in range(2):
+            attended_copy(0, k, side).wait_recv()
     project_out(0, list(range(lanes)), [])
     for copy in fetches + corners:
         copy.wait_send()
@@ -513,13 +518,15 @@
     for copy in w_copies:
         copy.wait_send()
     for k in range(1, lanes):
-        attended_copy(0, k).wait_send()
+        for side in range(2):
+            attended_copy(0, k, side).wait_send()
     for window in range(1, window_count):
         project_out(window, [0], [1] + list(reversed(range(2, lanes))))
 
     for window in range(1, window_count):
         for k in range(1, lanes):
-            attended_copy(window, k).wait_send()
+            for side in range(2):
+                attended_copy(window, k, side).wait_send()
 
 
 def share_levels(members, blocks, head_width):
@@ -571,8 +578,8 @@
             pltpu.SemaphoreType.DMA((pieces,)),
             pltpu.SemaphoreType.DMA((lanes, pieces)),
             pltpu.SemaphoreType.DMA((lanes, pieces)),
-            pltpu.SemaphoreType.DMA((window_count, lanes)),
-            pltpu.SemaphoreType.DMA((window_count, lanes)),
+            pltpu.SemaphoreType.DMA((window_count, lanes, 2)),
+            pltpu.SemaphoreType.DMA((window_count, lanes, 2)),
             pltpu.SemaphoreType.DMA((w_count,)),
             pltpu.SemaphoreType.DMA((w_count,)),
             pltpu.SemaphoreType.DMA((6,)),

time: 62 us -> 61.9 us (level)
  no operation moved by 1% of the time
where the time goes in v4:
time: 61.9 us; the launch traced here: 61.7 us
  Pallas kernels  60.6 us (98%)
  local copies, waits for them, and re-layouts  1.15 us (2%)
    pallas_call x1, Pallas kernels, on_device(): pl.pallas_call(functools.partial(layer_kernel, lanes, blocks, members), o...  60.6 us

profile of v4, /device:TPU:0, one launch (start us, length us, event | category | flops | bytes accessed | tf_op | source)
XLA Modules:
  0.0 61.7 jit_solution(14356863757022851624)
XLA Ops:
  0.0 60.6 %shard_map.73 = bf16[1,8,1,64,1536]{4,3,2,1,0:T(8,128)(2,1)S(1)} custom-call(f32[4]{0:T(128)} %scale_hbm.1, bf16[1,8,1,64,1536]{4,3,2,1,0:T(8,128)(2,1)} %x_ref.1, s32[1,32,64]{2,1,0:T(8,128)} %label_hbm.1, f32[1536]{0:T(1024)} %gain_hbm.1, f32[1536]{0:T(1024)} %bias_hbm.1, bf16[3,1536,384]{2,1,0:T(8,128)(2,1)} %wqkv_ref.1, bf16[384,1536]{1,0:T(8,128)(2,1)} %wout_ref.1), custom_call_target="tpu_custom_call" | custom-call | tf_op jit(solution)/shard_map/pallas_call | solution.py:555
  60.6 1.1 %copy.9 = bf16[1,8,1,64,1536]{4,3,2,1,0:T(8,128)(2,1)} copy(bf16[1,8,1,64,1536]{4,3,2,1,0:T(8,128)(2,1)S(1)} %shard_map.73) | data formatting | bytes 3145728
